TPU v7x, 32 devices: a whole 2x2x4 slice. The times are simulated.
32 devices in a mesh: gx: 8 (over z, x), gy: 4 (over y, core).
Axes of the slice: x: 2, y: 2, z: 4, core: 2. Of those that a mesh axis runs over, the one named last changes fastest.
Arguments:
- measures: bfloat16 [262144, 128], P(('gx', 'gy')), may hold values from -6 to 6
- row_keys: int32 [262144], P(('gx', 'gy')), may hold values from 0 to 16383, as said below
- orders: bfloat16 [16384, 128], P(('gx', 'gy')), may hold values from -6 to 6
- heavy_keys: int32 [64], replicated, may hold values from 0 to 16383, as said below
- key_slot: int32 [16384], replicated, may hold values from 0 to 16383, as said below
Outputs:
- result: bfloat16 [16384, 128], P(('gx', 'gy'))
- heavy_report: bfloat16 [64, 128], P(('gx', 'gy'))
- slot_rows: float32 [16384], P(('gx', 'gy'))
Inputs may be any that keep to these rules, and one draw needn't show every extreme that they name: `heavy_keys`: for each range block d, entries d * 2 to (d + 1) * 2 - 1 are distinct keys of d * 512 to (d + 1) * 512 - 1. `key_slot`: A permutation. Slot s belongs to owner s // 2048 and to quarter (s // 512) % q with q = 4. Key k lies in range block d = k // 512; every range block has exactly 64 keys with slots of each owner, all in quarter d % q. `row_keys`: in the rows of one device, among rows whose key is not heavy, at most 768 have slots of any one owner and at most 192 distinct keys have slots of any one owner; in every device both bounds are reached by some owner.
All inputs are finite; a program needn't handle non-finite values.
Results may differ from a plain program's by a relative error of at most 0.0021.
Values may be sent and summed in bfloat16 or wider, within the bound.
A program may use at most 64 MiB of HBM per device.

v0:
```python
import jax
import jax.numpy as jnp
from jax import lax
from jax.sharding import PartitionSpec as P


def block_length(total):
    return 2048 if total % 2048 == 0 else total


def one_hot_sums(values, targets, labels, weights):
    block_rows = block_length(targets.shape[0])
    blocks = targets.shape[0] // block_rows
    columns = values.shape[1]
    span = labels.shape[0]
    exact = values.dtype == jnp.float32

    def add_block(running, block_piece):
        block_values, block_targets, block_weights = block_piece
        matches = block_targets[:, None] == labels[None, :]
        onehot = matches.astype(values.dtype)
        if exact:
            product = lax.dot_general(
                onehot,
                block_values,
                (((0,), (0,)), ((), ())),
                precision=lax.Precision.HIGHEST,
                preferred_element_type=jnp.float32,
            )
        else:
            product = lax.dot_general(
                onehot, block_values, (((0,), (0,)), ((), ())), preferred_element_type=jnp.float32
            )
        totals = running[0] + product
        tallies = running[1] + jnp.sum(matches.astype(jnp.float32) * block_weights[:, None], axis=0)
        return ((totals, tallies), jnp.any(matches, axis=1))

    start_state = (jnp.zeros((span, columns), jnp.float32), jnp.zeros((span,), jnp.float32))
    pieces = (
        values.reshape(blocks, block_rows, columns),
        targets.reshape(blocks, block_rows),
        weights.reshape(blocks, block_rows),
    )
    (totals, tallies), matched = lax.scan(add_block, start_state, pieces)
    return (totals, tallies, matched.reshape(-1))


def body(measures, row_keys, orders, heavy_keys, key_slot):
    row_count, columns = measures.shape
    groups_x = lax.axis_size("gx")
    groups_y = lax.axis_size("gy")
    key_dev = orders.shape[0]
    own_slots = key_dev * groups_y
    heavy_total = heavy_keys.shape[0]
    heavy_each = heavy_total // (groups_x * groups_y)
    capacity = max(row_count // 32, 3 * row_count // (4 * groups_x))
    key_capacity = capacity // 4
    index_x = lax.axis_index("gx")
    index_y = lax.axis_index("gy")
    device = index_x * groups_y + index_y
    unit_rows = jnp.ones((row_count,), jnp.float32)
    heavy_part, heavy_count, heavy_flags = one_hot_sums(measures, row_keys, heavy_keys, unit_rows)
    slot_ids = key_slot[row_keys]
    owner_labels = jnp.arange(groups_x + 1, dtype=jnp.int32)
    own_base = index_x * own_slots
    own_labels = jnp.arange(own_slots, dtype=jnp.int32)
    sort_keys = jnp.where(heavy_flags, groups_x * own_slots, slot_ids)
    ordering = jnp.argsort(sort_keys, stable=True)
    sorted_slots = sort_keys[ordering]
    sorted_owner = sorted_slots // own_slots
    is_light = sorted_owner < groups_x
    fresh = (
        jnp.concatenate([jnp.ones((1,), bool), sorted_slots[1:] != sorted_slots[:-1]]) & is_light
    )
    distinct = jnp.cumsum(fresh.astype(jnp.int32)) - 1
    before = jnp.sum(
        (fresh[:, None] & (sorted_owner[:, None] < owner_labels[None, :])).astype(jnp.int32), axis=0
    )
    segments = groups_x * key_capacity
    segment = jnp.where(
        is_light, sorted_owner * key_capacity + distinct - before[sorted_owner], segments
    )
    row_segment = jnp.zeros((row_count,), jnp.int32).at[ordering].set(segment)
    partial_value, tallies, unused = one_hot_sums(
        measures, row_segment, jnp.arange(segments, dtype=jnp.int32), unit_rows
    )
    sent_slots = jnp.full((segments + 1,), -1, jnp.int32).at[segment].set(sorted_slots)[:segments]
    got_sums, got_tallies, got_slots = (
        lax.all_to_all(
            partial_value.reshape(groups_x, key_capacity, columns),
            "gx",
            split_axis=0,
            concat_axis=0,
            tiled=True,
        ),
        lax.all_to_all(
            tallies.reshape(groups_x, key_capacity), "gx", split_axis=0, concat_axis=0, tiled=True
        ),
        lax.all_to_all(
            sent_slots.reshape(groups_x, key_capacity),
            "gx",
            split_axis=0,
            concat_axis=0,
            tiled=True,
        ),
    )
    local_slot = got_slots.reshape(-1) - own_base
    local_slot = jnp.where(got_slots.reshape(-1) >= 0, local_slot, own_slots)
    light_totals, light_tallies, unused_too = one_hot_sums(
        got_sums.reshape(-1, columns), local_slot, own_labels, got_tallies.reshape(-1)
    )
    quarter_totals, quarter_tallies = (
        lax.psum_scatter(
            light_totals.reshape(groups_y, key_dev, columns), "gy", scatter_dimension=0, tiled=True
        ),
        lax.psum_scatter(
            light_tallies.reshape(groups_y, key_dev), "gy", scatter_dimension=0, tiled=True
        ),
    )
    slot_rows = quarter_tallies.reshape(key_dev)
    inverse = jnp.argsort(key_slot)
    held_keys = lax.dynamic_slice_in_dim(inverse, device * key_dev, key_dev)
    send_order = jnp.argsort(held_keys)
    per_peer = key_dev // groups_x
    moved_totals, moved_tallies = (
        lax.all_to_all(
            quarter_totals.reshape(key_dev, columns)[send_order].reshape(
                groups_x, per_peer, columns
            ),
            "gx",
            split_axis=0,
            concat_axis=0,
            tiled=True,
        ),
        lax.all_to_all(
            slot_rows[send_order].reshape(groups_x, per_peer),
            "gx",
            split_axis=0,
            concat_axis=0,
            tiled=True,
        ),
    )
    range_slots = lax.dynamic_slice_in_dim(key_slot, device * key_dev, key_dev)
    arrival = jnp.argsort(range_slots // own_slots, stable=True)
    placed = jnp.argsort(arrival)
    light_sum = moved_totals.reshape(key_dev, columns)[placed]
    light_count = moved_tallies.reshape(key_dev)[placed]
    my_heavy = lax.dynamic_slice_in_dim(heavy_keys, device * heavy_each, heavy_each)
    heavy_local = my_heavy - device * key_dev
    heavy_orders_here = orders[heavy_local]
    gathered = lax.all_gather(heavy_orders_here, ("gx", "gy"), axis=0, tiled=True)
    joined = heavy_part * gathered.astype(jnp.float32)
    joined_total, count_total = lax.psum((joined, heavy_count), ("gx", "gy"))
    mine_joined = lax.dynamic_slice_in_dim(joined_total, device * heavy_each, heavy_each)
    mine_count = lax.dynamic_slice_in_dim(count_total, device * heavy_each, heavy_each)
    heavy_value = mine_joined * lax.rsqrt(1.0 + mine_count)[:, None]
    light_value = orders.astype(jnp.float32) * light_sum * lax.rsqrt(1.0 + light_count)[:, None]
    placing = (heavy_local[:, None] == jnp.arange(key_dev, dtype=jnp.int32)[None, :]).astype(
        jnp.float32
    )
    heavy_full = jnp.sum(placing[:, :, None] * heavy_value[:, None, :], axis=0)
    result = (light_value + heavy_full).astype(jnp.bfloat16)
    return (result, heavy_value.astype(jnp.bfloat16), slot_rows)


def solution(mesh):
    return jax.shard_map(
        body,
        mesh=mesh,
        in_specs=(P(("gx", "gy"), None), P(("gx", "gy")), P(("gx", "gy"), None), P(), P()),
        out_specs=(P(("gx", "gy"), None), P(("gx", "gy"), None), P(("gx", "gy"))),
        check_vma=False,
    )
```

profile of v0, /device:TPU:0, one launch (start us, length us, event | category | flops | bytes accessed | tf_op | source)
XLA Modules:
  0.0 408.1 jit_solution(12164380390125514987)
XLA Ops:
  7.2 0.8 reshape.279
  8.0 0.8 fusion.26
  8.8 12.8 %while.33 = (s32[]{:T(128)}, f32[64,128]{1,0:T(8,128)S(1)}, f32[64]{0:T(128)S(1)}, pred[4,2048]{1,0:T(4,128)(4,1)S(1)}, s32[4,2048]{1,0:T(4,128)S(1)}, /*index=5...) while((s32[]{:T(128)}, f32[64,128]{1,0:T(8,128)S(1)}, f32[64]{0:T(128)S(1)}, ...), condition=%wide.region_3.4_spmd.clone, body=%wide.region_0.3_spmd.clone.sunk | while | flops 34355264 | bytes 643696 | solution.py:44
  8.8 1.3 convolution_add_fusion.2
  10.1 0.9 fusion.53
  11.0 0.8 compare_reduce_fusion.4
  12.0 1.3 convolution_add_fusion.2
  13.3 0.9 fusion.53
  14.2 0.8 compare_reduce_fusion.4
  15.2 1.3 convolution_add_fusion.2
  16.5 0.9 fusion.53
  17.4 0.8 compare_reduce_fusion.4
  18.4 1.3 convolution_add_fusion.2
  19.7 0.9 fusion.53
  20.6 0.8 compare_reduce_fusion.4
  21.6 45.5 %gather_fusion = s32[8192]{0:T(1024)S(1)} fusion(s32[16384]{0:T(1024)S(1)} %copy-done, s32[8192]{0:T(1024)S(1)} %fusion.26), kind=kCustom, calls=%fused_computation | custom fusion | bytes 98304 | tf_op jit(solution)/shard_map/gather | solution.py:63
  67.2 6.8 %sort.82 = (s32[8192]{0:T(1024)}, s32[8192]{0:T(1024)S(1)}) sort(s32[8192]{0:T(1024)S(1)} %broadcast_select_fusion.1, s32[8192]{0:T(1024)S(1)} %iota.43), dimensions={0}, to_apply=%region_4.5 | sort | flops 106496 | bytes 131072 | tf_op jit(solution)/shard_map/jit(argsort)/sort | solution.py:68
  73.9 45.5 %gather_fusion.1 = s32[8192]{0:T(1024)S(1)} fusion(s32[8192]{0:T(1024)S(1)} %broadcast_select_fusion.1, s32[8192]{0:T(1024)S(1)} %get-tuple-element.195), kind=kCustom, calls=%fused_computation.1 | custom fusion | bytes 98304 | tf_op jit(solution)/shard_map/gather | solution.py:69
  119.9 0.7 fusion.42
  120.6 4.7 %compare_select_fusion.3 = (s32[8192,1]{0,1:T(1,128)S(1)}, s32[8192,1]{0,1:T(1,128)S(1)}, s32[8192,1]{0,1:T(1,128)S(1)}) fusion(s32[]{:T(128)} %bitcast.7, s32[]{:T(128)} %bitcast.8, s32[]{:T(128)} %bitcast.9, s32[]{:T(128)} %bitcast.10, s32[]{:T(128)} %bitcast.11, s32[]{:T(128)} %bitcast.13, s32[]{:T(128)} %bitcast.12, s32[8192,1]{0,1:T(1,128)S(1)} %bitcast.83), kind=kLoop, calls=%fused_computation.49 | loop fusion | flops 245760 | bytes 131100 | tf_op jit(solution)/shard_map/gather | solution.py:81
  125.5 0.3 reduce-window.9
  126.1 1.4 fusion.28
  127.5 30.4 %scatter_custom_fusion = s32[1537]{0:T(1024)S(1)} fusion(s32[8192]{0:T(1024)S(1)} %bitcast.93, s32[8192]{0:T(1024)S(1)} %gather_fusion.1, s32[]{:T(128)} %constant.66.clone.1), kind=kCustom, calls=%fused_computation.106 | custom fusion | bytes 6152 | tf_op jit(solution)/shard_map/scatter | solution.py:87
  158.0 0.7 all_to_all.24
  158.7 7.3 %all-to-all-start = ((s32[8,1,192]{2,1,0:T(1,128)}), s32[8,1,192]{2,1,0:T(1,128)S(1)}, u32[]{:S(2)}, u32[]{:S(2)}) async-start(s32[8,1,192]{2,1,0:T(1,128)} %all_to_all.24), calls=%async_computation | async-start | bytes 16384 | tf_op jit(solution)/shard_map/all_to_all | solution.py:99
  165.9 30.7 %scatter_custom_fusion.1 = s32[8192]{0:T(1024)S(1)} fusion(s32[8192]{0:T(1024)S(1)} %get-tuple-element.196, s32[8192]{0:T(1024)S(1)} %get-tuple-element.185, s32[]{:T(128)} %constant.68.clone.1), kind=kCustom, calls=%fused_computation.95 | custom fusion | bytes 32772 | tf_op jit(solution)/shard_map/scatter | solution.py:83
  196.6 30.3 %while.34 = (s32[]{:T(128)}, f32[1536,128]{1,0:T(8,128)}, f32[1536]{0:T(1024)S(1)}, s32[4,2048]{1,0:T(4,128)S(1)}, bf16[4,2048,128]{2,1,0:T(8,128)(2,1)}, /*index=5*/s32[]{:T(128)}, s32[]{:T(128)}) while((s32[]{:T(128)}, f32[1536,128]{1,0:T(8,128)}, f32[1536]{0:T(1024)S(1)}, s32[4,2048]{1,0:T(4,128)S(1)}, ...), condition=%wide.region_12.13_spmd.clone, body=%wide.region_10.12_spmd.clone.sunk | while | flops 818284032 | bytes 2155100 | solution.py:44
  196.7 5.7 %fusion.56 = f32[1536,128]{1,0:T(8,128)} fusion(s32[2048]{0:T(1024)S(1)} %bitcast.85, f32[1536,128]{1,0:T(8,128)} %get-tuple-element.315, bf16[4,2048,128]{2,1,0:T(8,128)(2,1)} %get-tuple-element.325, s32[]{:T(128)} %get-tuple-element.314, pred[]{:T(512)S(6)} %compare.110), kind=kOutput, calls=%fused_computation.28.clone.1 | convolution fusion | flops 808845312 | bytes 2105857 | tf_op jit(solution)/shard_map/while/body/eval_jaxpr/dot_general | solution.py:31
  202.3 1.7 fusion.57
  204.1 5.9 %fusion.56 = f32[1536,128]{1,0:T(8,128)} fusion(s32[2048]{0:T(1024)S(1)} %bitcast.85, f32[1536,128]{1,0:T(8,128)} %get-tuple-element.315, bf16[4,2048,128]{2,1,0:T(8,128)(2,1)} %get-tuple-element.325, s32[]{:T(128)} %get-tuple-element.314, pred[]{:T(512)S(6)} %compare.110), kind=kOutput, calls=%fused_computation.28.clone.1 | convolution fusion | flops 808845312 | bytes 2105857 | tf_op jit(solution)/shard_map/while/body/eval_jaxpr/dot_general | solution.py:31
  210.0 1.7 fusion.57
  211.7 5.9 %fusion.56 = f32[1536,128]{1,0:T(8,128)} fusion(s32[2048]{0:T(1024)S(1)} %bitcast.85, f32[1536,128]{1,0:T(8,128)} %get-tuple-element.315, bf16[4,2048,128]{2,1,0:T(8,128)(2,1)} %get-tuple-element.325, s32[]{:T(128)} %get-tuple-element.314, pred[]{:T(512)S(6)} %compare.110), kind=kOutput, calls=%fused_computation.28.clone.1 | convolution fusion | flops 808845312 | bytes 2105857 | tf_op jit(solution)/shard_map/while/body/eval_jaxpr/dot_general | solution.py:31
  217.6 1.7 fusion.57
  219.3 5.9 %fusion.56 = f32[1536,128]{1,0:T(8,128)} fusion(s32[2048]{0:T(1024)S(1)} %bitcast.85, f32[1536,128]{1,0:T(8,128)} %get-tuple-element.315, bf16[4,2048,128]{2,1,0:T(8,128)(2,1)} %get-tuple-element.325, s32[]{:T(128)} %get-tuple-element.314, pred[]{:T(512)S(6)} %compare.110), kind=kOutput, calls=%fused_computation.28.clone.1 | convolution fusion | flops 808845312 | bytes 2105857 | tf_op jit(solution)/shard_map/while/body/eval_jaxpr/dot_general | solution.py:31
  225.2 1.7 fusion.57
  226.9 6.0 %all-to-all-start.1 = ((f32[8,192,128]{2,1,0:T(8,128)}), f32[8,192,128]{2,1,0:T(8,128)S(1)}, u32[]{:S(2)}, u32[]{:S(2)}) async-start(f32[8,192,128]{2,1,0:T(8,128)} %bitcast.18), calls=%async_computation.1 | async-start | bytes 1572864 | tf_op jit(solution)/shard_map/all_to_all | solution.py:89
  233.1 19.5 %all-to-all-done.1 = f32[8,192,128]{2,1,0:T(8,128)S(1)} async-done(((f32[8,192,128]{2,1,0:T(8,128)}), f32[8,192,128]{2,1,0:T(8,128)S(1)}, u32[]{:S(2)}, u32[]{:S(2)}) %all-to-all-start.1) | async-done | bytes 786464 | tf_op jit(solution)/shard_map/all_to_all | solution.py:89
  252.6 6.3 %fusion.18 = f32[4,512,128]{2,1,0:T(8,128)} fusion(f32[1536,128,1]{1,0,2:T(8,128)S(1)} %bitcast.84, s32[4,512]{1,0:T(4,128)S(1)} %multiply_add_fusion, s32[1536]{0:T(1024)S(1)} %select_n.113), kind=kOutput, calls=%fused_computation.36 | convolution fusion | flops 4834983936 | bytes 1849344 | tf_op jit(solution)/shard_map/while/body/eval_jaxpr/dot_general | solution.py:23
  258.9 0.7 all_to_all.28
  259.6 3.5 all-to-all-start.3
  263.1 7.8 %sort.83 = (s32[16384]{0:T(1024)}, s32[16384]{0:T(1024)S(1)}) sort(s32[16384]{0:T(1024)S(1)} %copy-done, s32[16384]{0:T(1024)S(1)} %iota.45), dimensions={0}, to_apply=%region_14.15 | sort | flops 229376 | bytes 262144 | tf_op jit(solution)/shard_map/jit(argsort)/sort | solution.py:121
  270.9 0.6 dynamic-slice.1
  271.5 3.8 sort.84
  275.4 3.8 sort.85
  279.2 3.8 sort.86
  283.0 0.6 gather_fusion.6
  283.6 42.0 %all-gather.1 = bf16[32,2,128]{2,1,0:T(2,128)(2,1)S(1)} all-gather(bf16[1,2,128]{2,1,0:T(2,128)(2,1)S(1)} %bitcast.95), channel_id=2, replica_groups=mesh['gx'=8,'gy'=4] {'gx','gy'}, dimensions={0}, use_global_device_ids=true | all-gather | bytes 16896 | tf_op jit(solution)/shard_map/all_gather | solution.py:151
  325.7 37.2 %all-reduce.1 = (f32[64,128]{1,0:T(8,128)S(1)}, f32[64]{0:T(128)S(1)}) all-reduce(f32[64,128]{1,0:T(8,128)S(1)} %convert_multiply_fusion, f32[64]{0:T(128)S(1)} %get-tuple-element.110), channel_id=1, replica_groups=mesh['gx'=8,'gy'=4] {'gx','gy'}, use_global_device_ids=true, to_apply=%region_20.21 | all-reduce | flops 8256 | bytes 66048 | tf_op jit(solution)/shard_map/psum | solution.py:153
  362.9 1.8 select_reduce_fusion
  364.8 5.9 %all-reduce = f32[4,512]{1,0:T(4,128)S(1)} all-reduce(f32[4,512]{1,0:T(4,128)S(1)} %reshape.288), channel_id=4, replica_groups=mesh['gx'=8,'gy'=4] {'gy'}, use_global_device_ids=true, to_apply=%region_19.20.clone | all-reduce | flops 2048 | bytes 16384
  370.7 0.7 constant_dynamic-slice_fusion.2
  371.4 3.5 gather_fusion.4
  374.9 0.7 all_to_all.30
  375.5 5.9 %all-to-all-start.4 = ((f32[8,1,64]{2,1,0:T(1,128)}), f32[8,1,64]{2,1,0:T(1,128)S(1)}, u32[]{:S(2)}, u32[]{:S(2)}) async-start(f32[8,1,64]{2,1,0:T(1,128)} %all_to_all.30), calls=%async_computation.5 | async-start | bytes 8192 | tf_op jit(solution)/shard_map/all_to_all | solution.py:135
  381.5 2.6 gather_fusion.2
  384.1 3.7 all-to-all-done.4
  387.8 3.4 all-to-all-start.2
  391.2 0.6 fusion.41
  392.0 0.5 broadcast.477
  392.5 0.7 reduce.12
  393.3 3.5 gather_fusion.5
  396.8 2.6 all-to-all-done.2
  399.4 1.0 gather_fusion.3
  400.4 0.8 add_convert_fusion
  (82 shorter events, 2.6 us)
Async XLA Ops:
  7.2 14.4 %copy-start = (s32[16384]{0:T(1024)S(1)}, s32[16384]{0:T(1024)}, u32[]{:S(2)}) copy-start(s32[16384]{0:T(1024)} %param.13) | copy-start | bytes 196612
  158.7 68.2 %all-to-all-start = ((s32[8,1,192]{2,1,0:T(1,128)}), s32[8,1,192]{2,1,0:T(1,128)S(1)}, u32[]{:S(2)}, u32[]{:S(2)}) async-start(s32[8,1,192]{2,1,0:T(1,128)} %all_to_all.24), calls=%async_computation | async-start | bytes 16384 | tf_op jit(solution)/shard_map/all_to_all | solution.py:99
  226.9 25.7 %all-to-all-start.1 = ((f32[8,192,128]{2,1,0:T(8,128)}), f32[8,192,128]{2,1,0:T(8,128)S(1)}, u32[]{:S(2)}, u32[]{:S(2)}) async-start(f32[8,192,128]{2,1,0:T(8,128)} %bitcast.18), calls=%async_computation.1 | async-start | bytes 1572864 | tf_op jit(solution)/shard_map/all_to_all | solution.py:89
  232.9 148.6 %reduce-scatter.2.cloned.1.call-start = ((), (), s32[]{:S(2)}) async-start(), calls=%async_computation.6 | async-start | bytes 1310720 | tf_op jit(solution)/shard_map/reduce_scatter | solution.py:113
  252.6 18.3 %copy-start.4 = (u32[32]{0:T(128)S(1)}, u32[32]{0:T(128)}, u32[]{:S(2)}) copy-start(u32[32]{0:T(128)} %constant.146) | copy-start | bytes 388
  252.6 30.3 %copy-start.3 = (s32[64]{0:T(128)S(1)}, s32[64]{0:T(128)}, u32[]{:S(2)}) copy-start(s32[64]{0:T(128)} %get-tuple-element.335) | copy-start | bytes 772
  252.6 30.4 %copy-start.2 = (bf16[512,128]{1,0:T(8,128)(2,1)S(1)}, bf16[512,128]{1,0:T(8,128)(2,1)}, u32[]{:S(2)}) copy-start(bf16[512,128]{1,0:T(8,128)(2,1)} %param.11) | copy-start | bytes 393220
  259.6 103.3 %all-to-all-start.3 = ((f32[8,1,192]{2,1,0:T(1,128)}), f32[8,1,192]{2,1,0:T(1,128)S(1)}, u32[]{:S(2)}, u32[]{:S(2)}) async-start(f32[8,1,192]{2,1,0:T(1,128)} %all_to_all.28), calls=%async_computation.4 | async-start | bytes 16384 | tf_op jit(solution)/shard_map/all_to_all | solution.py:96
  371.3 12.7 %copy-start.1 = (f32[1,512]{1,0:T(1,128)}, f32[1,512]{1,0:T(1,128)S(1)}, u32[]{:S(2)}) copy-start(f32[1,512]{1,0:T(1,128)S(1)} %constant_dynamic-slice_fusion.2) | copy-start | bytes 6148
  375.5 12.3 %all-to-all-start.4 = ((f32[8,1,64]{2,1,0:T(1,128)}), f32[8,1,64]{2,1,0:T(1,128)S(1)}, u32[]{:S(2)}, u32[]{:S(2)}) async-start(f32[8,1,64]{2,1,0:T(1,128)} %all_to_all.30), calls=%async_computation.5 | async-start | bytes 8192 | tf_op jit(solution)/shard_map/all_to_all | solution.py:135
  387.8 11.6 %all-to-all-start.2 = ((f32[8,64,128]{2,1,0:T(8,128)}), f32[8,64,128]{2,1,0:T(8,128)S(1)}, u32[]{:S(2)}, u32[]{:S(2)}) async-start(f32[8,64,128]{2,1,0:T(8,128)} %bitcast.22), calls=%async_computation.3 | async-start | bytes 524288 | tf_op jit(solution)/shard_map/all_to_all | solution.py:126
Sparse Core Ops, SparseCore 0:
  259.0 23.9 reduce-scatter.1
where the time goes:
time: 409 us; the launch traced here: 408 us
  local copies, waits for them, and re-layouts  170 us (42%)
  blocking collectives  85 us (21%)
  other arithmetic  51.7 us (13%)
  matrix products  35 us (9%)
  starting transfers between devices  26.1 us (6%)
  waiting for transfers between devices  25.9 us (6%)
  between operations  14.4 us (4%)
    gather x1, local copies, waits for them, and re-layouts, body(): slot_ids = key_slot[row_keys]  45.5 us
    gather x1, local copies, waits for them, and re-layouts, body(): sorted_slots = sort_keys[ordering]  45.5 us
    all_gather x1, blocking collectives, body(): lax.all_gather(heavy_orders_here, ('gx', 'gy'), axis=0, tiled=True)  42 us
    psum x1, blocking collectives, body(): joined_total, count_total = lax.psum((joined, heavy_count), ('gx', 'gy'))  37.2 us
    scatter x1, local copies, waits for them, and re-layouts, body(): row_segment = jnp.zeros((row_count,), jnp.int32).at[ordering].set(segment)  30.7 us
    scatter x1, local copies, waits for them, and re-layouts, body(): jnp.full((segments + 1,), -1, jnp.int32).at[segment].set(sorted_slots)  30.4 us
    dot_general x8, matrix products, add_block(): lax.dot_general(onehot, block_values, (((0,), (0,)), ((), ())), preferred...  28.7 us
    all_to_all x1, waiting for transfers between devices, body(): lax.all_to_all(partial_value.reshape(groups_x, key_capacity, columns), 'g...  19.5 us
  transfers between devices with their start and end apart: 6, of which 3 were waited for; matrix products, arithmetic and copies ran while one was open for 23% of the time, Pallas kernels for 0%

commit v1 on v0

--- a/solution.py
+++ b/solution.py
@@ -148,7 +148,12 @@
     my_heavy = lax.dynamic_slice_in_dim(heavy_keys, device * heavy_each, heavy_each)
     heavy_local = my_heavy - device * key_dev
     heavy_orders_here = orders[heavy_local]
-    gathered = lax.all_gather(heavy_orders_here, ("gx", "gy"), axis=0, tiled=True)
+    gathered = jnp.concatenate(
+        lax.all_to_all(
+            jnp.stack([heavy_orders_here] * lax.axis_size(("gx", "gy"))), ("gx", "gy"), 0, 0
+        ),
+        axis=0,
+    )
     joined = heavy_part * gathered.astype(jnp.float32)
     joined_total, count_total = lax.psum((joined, heavy_count), ("gx", "gy"))
     mine_joined = lax.dynamic_slice_in_dim(joined_total, device * heavy_each, heavy_each)

time: 409 us -> 359 us (0.88)
  blocking collectives: 85 us -> 46.9 us
  waiting for transfers between devices: 25.9 us -> 8.2 us
  starting transfers between devices: 26.1 us -> 31.3 us
    all_gather x1 -> x0, blocking collectives: 42 us -> none  [body(): lax.all_gather(heavy_orders_here, ('gx', 'gy'), axis=0, tiled=True)]
    all_to_all x1, waiting for transfers between devices: 19.5 us -> 0.01 us  [body(): lax.all_to_all(partial_value.reshape(groups_x, key_capacity, columns), 'g...]
  transfers between devices with their start and end apart: 6 -> 7, of which waited for: 3 -> 2; matrix products, arithmetic and copies ran while one was open for 23% -> 28% of each run, Pallas kernels for 0% -> 0%
where the time goes in v1:
time: 359 us; the launch traced here: 358 us
  local copies, waits for them, and re-layouts  170 us (47%)
  other arithmetic  51.7 us (14%)
  blocking collectives  46.9 us (13%)
  matrix products  35 us (10%)
  starting transfers between devices  31.3 us (9%)
  between operations  14.4 us (4%)
  waiting for transfers between devices  8.2 us (2%)
    gather x1, local copies, waits for them, and re-layouts, body(): slot_ids = key_slot[row_keys]  45.5 us
    gather x1, local copies, waits for them, and re-layouts, body(): sorted_slots = sort_keys[ordering]  45.5 us
    psum x1, blocking collectives, body(): joined_total, count_total = lax.psum((joined, heavy_count), ('gx', 'gy'))  41.1 us
    scatter x1, local copies, waits for them, and re-layouts, body(): row_segment = jnp.zeros((row_count,), jnp.int32).at[ordering].set(segment)  30.7 us
    scatter x1, local copies, waits for them, and re-layouts, body(): jnp.full((segments + 1,), -1, jnp.int32).at[segment].set(sorted_slots)  30.4 us
    dot_general x8, matrix products, add_block(): lax.dot_general(onehot, block_values, (((0,), (0,)), ((), ())), preferred...  28.7 us
    reduce_sum x9, other arithmetic, add_block(): jnp.sum(matches.astype(jnp.float32) * block_weights[:, None], axis=0)  12 us
    sort x1, other arithmetic, body(): inverse = jnp.argsort(key_slot)  7.75 us
  transfers between devices with their start and end apart: 7, of which 2 were waited for; matrix products, arithmetic and copies ran while one was open for 28% of the time, Pallas kernels for 0%

profile of v1, /device:TPU:0, one launch (start us, length us, event | category | flops | bytes accessed | tf_op | source)
XLA Modules:
  0.0 358.1 jit_solution(13248596491475661887)
XLA Ops:
  7.2 0.8 reshape.284
  8.0 0.8 fusion.26
  8.8 12.8 %while.33 = (s32[]{:T(128)}, f32[64,128]{1,0:T(8,128)S(1)}, f32[64]{0:T(128)S(1)}, pred[4,2048]{1,0:T(4,128)(4,1)S(1)}, s32[4,2048]{1,0:T(4,128)S(1)}, /*index=5...) while((s32[]{:T(128)}, f32[64,128]{1,0:T(8,128)S(1)}, f32[64]{0:T(128)S(1)}, ...), condition=%wide.region_3.4_spmd.clone, body=%wide.region_0.3_spmd.clone.sunk | while | flops 34355264 | bytes 643696 | solution.py:44
  8.8 1.3 convolution_add_fusion.2
  10.1 0.9 fusion.53
  11.0 0.8 compare_reduce_fusion.4
  12.0 1.3 convolution_add_fusion.2
  13.3 0.9 fusion.53
  14.2 0.8 compare_reduce_fusion.4
  15.2 1.3 convolution_add_fusion.2
  16.5 0.9 fusion.53
  17.4 0.8 compare_reduce_fusion.4
  18.4 1.3 convolution_add_fusion.2
  19.7 0.9 fusion.53
  20.6 0.8 compare_reduce_fusion.4
  21.6 45.5 %gather_fusion = s32[8192]{0:T(1024)S(1)} fusion(s32[16384]{0:T(1024)S(1)} %copy-done, s32[8192]{0:T(1024)S(1)} %fusion.26), kind=kCustom, calls=%fused_computation | custom fusion | bytes 98304 | tf_op jit(solution)/shard_map/gather | solution.py:63
  67.2 6.8 %sort.82 = (s32[8192]{0:T(1024)}, s32[8192]{0:T(1024)S(1)}) sort(s32[8192]{0:T(1024)S(1)} %broadcast_select_fusion.1, s32[8192]{0:T(1024)S(1)} %iota.43), dimensions={0}, to_apply=%region_4.5 | sort | flops 106496 | bytes 131072 | tf_op jit(solution)/shard_map/jit(argsort)/sort | solution.py:68
  73.9 45.5 %gather_fusion.1 = s32[8192]{0:T(1024)S(1)} fusion(s32[8192]{0:T(1024)S(1)} %broadcast_select_fusion.1, s32[8192]{0:T(1024)S(1)} %get-tuple-element.195), kind=kCustom, calls=%fused_computation.1 | custom fusion | bytes 98304 | tf_op jit(solution)/shard_map/gather | solution.py:69
  119.9 0.7 fusion.42
  120.6 4.7 %compare_select_fusion.3 = (s32[8192,1]{0,1:T(1,128)S(1)}, s32[8192,1]{0,1:T(1,128)S(1)}, s32[8192,1]{0,1:T(1,128)S(1)}) fusion(s32[]{:T(128)} %bitcast.7, s32[]{:T(128)} %bitcast.8, s32[]{:T(128)} %bitcast.9, s32[]{:T(128)} %bitcast.10, s32[]{:T(128)} %bitcast.11, s32[]{:T(128)} %bitcast.13, s32[]{:T(128)} %bitcast.12, s32[8192,1]{0,1:T(1,128)S(1)} %bitcast.82), kind=kLoop, calls=%fused_computation.49 | loop fusion | flops 245760 | bytes 131100 | tf_op jit(solution)/shard_map/gather | solution.py:81
  125.5 0.3 reduce-window.9
  126.1 1.4 fusion.28
  127.5 30.4 %scatter_custom_fusion = s32[1537]{0:T(1024)S(1)} fusion(s32[8192]{0:T(1024)S(1)} %bitcast.92, s32[8192]{0:T(1024)S(1)} %gather_fusion.1, s32[]{:T(128)} %constant.66.clone.1), kind=kCustom, calls=%fused_computation.106 | custom fusion | bytes 6152 | tf_op jit(solution)/shard_map/scatter | solution.py:87
  158.0 0.7 all_to_all.27
  158.7 7.3 %all-to-all-start = ((s32[8,1,192]{2,1,0:T(1,128)}), s32[8,1,192]{2,1,0:T(1,128)S(1)}, u32[]{:S(2)}, u32[]{:S(2)}) async-start(s32[8,1,192]{2,1,0:T(1,128)} %all_to_all.27), calls=%async_computation | async-start | bytes 16384 | tf_op jit(solution)/shard_map/all_to_all | solution.py:99
  165.9 30.7 %scatter_custom_fusion.1 = s32[8192]{0:T(1024)S(1)} fusion(s32[8192]{0:T(1024)S(1)} %get-tuple-element.196, s32[8192]{0:T(1024)S(1)} %get-tuple-element.185, s32[]{:T(128)} %constant.68.clone.1), kind=kCustom, calls=%fused_computation.95 | custom fusion | bytes 32772 | tf_op jit(solution)/shard_map/scatter | solution.py:83
  196.6 30.3 %while.34 = (s32[]{:T(128)}, f32[1536,128]{1,0:T(8,128)}, f32[1536]{0:T(1024)S(1)}, s32[4,2048]{1,0:T(4,128)S(1)}, bf16[4,2048,128]{2,1,0:T(8,128)(2,1)}, /*index=5*/s32[]{:T(128)}, s32[]{:T(128)}) while((s32[]{:T(128)}, f32[1536,128]{1,0:T(8,128)}, f32[1536]{0:T(1024)S(1)}, s32[4,2048]{1,0:T(4,128)S(1)}, ...), condition=%wide.region_12.13_spmd.clone, body=%wide.region_10.12_spmd.clone.sunk | while | flops 818284032 | bytes 2155100 | solution.py:44
  196.7 5.7 %fusion.56 = f32[1536,128]{1,0:T(8,128)} fusion(s32[2048]{0:T(1024)S(1)} %bitcast.84, f32[1536,128]{1,0:T(8,128)} %get-tuple-element.315, bf16[4,2048,128]{2,1,0:T(8,128)(2,1)} %get-tuple-element.325, s32[]{:T(128)} %get-tuple-element.314, pred[]{:T(512)S(6)} %compare.110), kind=kOutput, calls=%fused_computation.28.clone.1 | convolution fusion | flops 808845312 | bytes 2105857 | tf_op jit(solution)/shard_map/while/body/eval_jaxpr/dot_general | solution.py:31
  202.3 1.7 fusion.57
  204.1 5.9 %fusion.56 = f32[1536,128]{1,0:T(8,128)} fusion(s32[2048]{0:T(1024)S(1)} %bitcast.84, f32[1536,128]{1,0:T(8,128)} %get-tuple-element.315, bf16[4,2048,128]{2,1,0:T(8,128)(2,1)} %get-tuple-element.325, s32[]{:T(128)} %get-tuple-element.314, pred[]{:T(512)S(6)} %compare.110), kind=kOutput, calls=%fused_computation.28.clone.1 | convolution fusion | flops 808845312 | bytes 2105857 | tf_op jit(solution)/shard_map/while/body/eval_jaxpr/dot_general | solution.py:31
  210.0 1.7 fusion.57
  211.7 5.9 %fusion.56 = f32[1536,128]{1,0:T(8,128)} fusion(s32[2048]{0:T(1024)S(1)} %bitcast.84, f32[1536,128]{1,0:T(8,128)} %get-tuple-element.315, bf16[4,2048,128]{2,1,0:T(8,128)(2,1)} %get-tuple-element.325, s32[]{:T(128)} %get-tuple-element.314, pred[]{:T(512)S(6)} %compare.110), kind=kOutput, calls=%fused_computation.28.clone.1 | convolution fusion | flops 808845312 | bytes 2105857 | tf_op jit(solution)/shard_map/while/body/eval_jaxpr/dot_general | solution.py:31
  217.6 1.7 fusion.57
  219.3 5.9 %fusion.56 = f32[1536,128]{1,0:T(8,128)} fusion(s32[2048]{0:T(1024)S(1)} %bitcast.84, f32[1536,128]{1,0:T(8,128)} %get-tuple-element.315, bf16[4,2048,128]{2,1,0:T(8,128)(2,1)} %get-tuple-element.325, s32[]{:T(128)} %get-tuple-element.314, pred[]{:T(512)S(6)} %compare.110), kind=kOutput, calls=%fused_computation.28.clone.1 | convolution fusion | flops 808845312 | bytes 2105857 | tf_op jit(solution)/shard_map/while/body/eval_jaxpr/dot_general | solution.py:31
  225.2 1.7 fusion.57
  226.9 6.0 %all-to-all-start.1 = ((f32[8,192,128]{2,1,0:T(8,128)}), f32[8,192,128]{2,1,0:T(8,128)S(1)}, u32[]{:S(2)}, u32[]{:S(2)}) async-start(f32[8,192,128]{2,1,0:T(8,128)} %bitcast.18), calls=%async_computation.1 | async-start | bytes 1572864 | tf_op jit(solution)/shard_map/all_to_all | solution.py:89
  232.9 0.7 all_to_all.31
  233.6 7.7 %sort.83 = (s32[16384]{0:T(1024)}, s32[16384]{0:T(1024)S(1)}) sort(s32[16384]{0:T(1024)S(1)} %copy-done, s32[16384]{0:T(1024)S(1)} %iota.45), dimensions={0}, to_apply=%region_14.15 | sort | flops 229376 | bytes 262144 | tf_op jit(solution)/shard_map/jit(argsort)/sort | solution.py:121
  241.4 3.8 %sort.84 = (s32[512]{0:T(512)}, s32[512]{0:T(512)S(1)}) sort(s32[512]{0:T(512)S(1)} %dynamic_slice.41, s32[512]{0:T(512)S(1)} %iota.46), dimensions={0}, to_apply=%region_15.16 | sort | flops 4608 | bytes 8192 | tf_op jit(solution)/shard_map/jit(argsort)/sort | solution.py:123
  245.3 3.8 %sort.85 = (s32[512]{0:T(512)}, s32[512]{0:T(512)S(1)}) sort(s32[512]{0:T(512)S(1)} %add_select_fusion.2, s32[512]{0:T(512)S(1)} %iota.47), dimensions={0}, to_apply=%region_16.17 | sort | flops 4608 | bytes 8192 | tf_op jit(solution)/shard_map/jit(argsort)/sort | solution.py:144
  249.1 3.8 %sort.86 = (s32[512]{0:T(512)}, s32[512]{0:T(512)S(1)}) sort(s32[512]{0:T(512)S(1)} %get-tuple-element.106, s32[512]{0:T(512)S(1)} %iota.48), dimensions={0}, to_apply=%region_17.18 | sort | flops 4608 | bytes 8192 | tf_op jit(solution)/shard_map/jit(argsort)/sort | solution.py:145
  252.9 6.0 %all-to-all-start.3 = ((f32[8,1,192]{2,1,0:T(1,128)}), f32[8,1,192]{2,1,0:T(1,128)S(1)}, u32[]{:S(2)}, u32[]{:S(2)}) async-start(f32[8,1,192]{2,1,0:T(1,128)} %all_to_all.31), calls=%async_computation.4 | async-start | bytes 16384 | tf_op jit(solution)/shard_map/all_to_all | solution.py:96
  259.2 6.3 %fusion.18 = f32[4,512,128]{2,1,0:T(8,128)} fusion(f32[1536,128,1]{1,0,2:T(8,128)S(1)} %bitcast.83, s32[4,512]{1,0:T(4,128)S(1)} %multiply_add_fusion, s32[1536]{0:T(1024)S(1)} %select_n.113), kind=kOutput, calls=%fused_computation.36 | convolution fusion | flops 4834983936 | bytes 1849344 | tf_op jit(solution)/shard_map/while/body/eval_jaxpr/dot_general | solution.py:23
  265.7 0.6 dynamic-slice.1
  266.4 1.8 select_reduce_fusion
  268.3 5.8 %all-reduce = f32[4,512]{1,0:T(4,128)S(1)} all-reduce(f32[4,512]{1,0:T(4,128)S(1)} %reshape.293), channel_id=3, replica_groups=mesh['gx'=8,'gy'=4] {'gy'}, use_global_device_ids=true, to_apply=%region_19.20.clone | all-reduce | flops 2048 | bytes 16384
  274.0 0.7 constant_dynamic-slice_fusion.2
  274.7 3.5 gather_fusion.4
  278.2 0.7 all_to_all.33
  278.9 5.7 %all-to-all-start.4 = ((f32[8,1,64]{2,1,0:T(1,128)}), f32[8,1,64]{2,1,0:T(1,128)S(1)}, u32[]{:S(2)}, u32[]{:S(2)}) async-start(f32[8,1,64]{2,1,0:T(1,128)} %all_to_all.33), calls=%async_computation.5 | async-start | bytes 8192 | tf_op jit(solution)/shard_map/all_to_all | solution.py:135
  284.6 0.6 gather_fusion.6
  285.2 5.8 %all-to-all-done.4 = f32[8,1,64]{2,1,0:T(1,128)S(1)} async-done(((f32[8,1,64]{2,1,0:T(1,128)}), f32[8,1,64]{2,1,0:T(1,128)S(1)}, u32[]{:S(2)}, u32[]{:S(2)}) %all-to-all-start.4) | async-done | bytes 2080 | tf_op jit(solution)/shard_map/all_to_all | solution.py:135
  291.0 0.6 stack.2
  291.6 2.5 all-to-all-start.5
  294.2 0.5 broadcast.479
  294.7 0.7 reduce.12
  295.5 3.5 gather_fusion.5
  299.0 2.3 all-to-all-done.5
  301.3 2.6 gather_fusion.2
  303.9 3.5 all-to-all-start.2
  307.4 41.1 %all-reduce.1 = (f32[64,128]{1,0:T(8,128)S(1)}, f32[64]{0:T(128)S(1)}) all-reduce(f32[64,128]{1,0:T(8,128)S(1)} %convert_multiply_fusion, f32[64]{0:T(128)S(1)} %get-tuple-element.110), channel_id=1, replica_groups=mesh['gx'=8,'gy'=4] {'gx','gy'}, use_global_device_ids=true, to_apply=%region_20.21 | all-reduce | flops 8256 | bytes 66048 | tf_op jit(solution)/shard_map/psum | solution.py:158
  348.6 0.6 fusion.41
  349.5 1.0 gather_fusion.3
  350.5 0.8 add_convert_fusion
  (84 shorter events, 2.8 us)
Async XLA Ops:
  7.2 14.4 %copy-start = (s32[16384]{0:T(1024)S(1)}, s32[16384]{0:T(1024)}, u32[]{:S(2)}) copy-start(s32[16384]{0:T(1024)} %param.13) | copy-start | bytes 196612
  158.7 68.2 %all-to-all-start = ((s32[8,1,192]{2,1,0:T(1,128)}), s32[8,1,192]{2,1,0:T(1,128)S(1)}, u32[]{:S(2)}, u32[]{:S(2)}) async-start(s32[8,1,192]{2,1,0:T(1,128)} %all_to_all.27), calls=%async_computation | async-start | bytes 16384 | tf_op jit(solution)/shard_map/all_to_all | solution.py:99
  226.9 26.0 %all-to-all-start.1 = ((f32[8,192,128]{2,1,0:T(8,128)}), f32[8,192,128]{2,1,0:T(8,128)S(1)}, u32[]{:S(2)}, u32[]{:S(2)}) async-start(f32[8,192,128]{2,1,0:T(8,128)} %bitcast.18), calls=%async_computation.1 | async-start | bytes 1572864 | tf_op jit(solution)/shard_map/all_to_all | solution.py:89
  252.9 13.4 %all-to-all-start.3 = ((f32[8,1,192]{2,1,0:T(1,128)}), f32[8,1,192]{2,1,0:T(1,128)S(1)}, u32[]{:S(2)}, u32[]{:S(2)}) async-start(f32[8,1,192]{2,1,0:T(1,128)} %all_to_all.31), calls=%async_computation.4 | async-start | bytes 16384 | tf_op jit(solution)/shard_map/all_to_all | solution.py:96
  258.9 42.4 %reduce-scatter.2.cloned.1.call-start = ((), (), s32[]{:S(2)}) async-start(), calls=%async_computation.7 | async-start | bytes 1310720 | tf_op jit(solution)/shard_map/reduce_scatter | solution.py:113
  259.2 6.3 %copy-start.3 = (s32[64]{0:T(128)S(1)}, s32[64]{0:T(128)}, u32[]{:S(2)}) copy-start(s32[64]{0:T(128)} %get-tuple-element.335) | copy-start | bytes 772
  259.2 6.5 %copy-start.4 = (u32[32]{0:T(128)S(1)}, u32[32]{0:T(128)}, u32[]{:S(2)}) copy-start(u32[32]{0:T(128)} %constant.146) | copy-start | bytes 388
  265.5 19.1 %copy-start.2 = (bf16[512,128]{1,0:T(8,128)(2,1)S(1)}, bf16[512,128]{1,0:T(8,128)(2,1)}, u32[]{:S(2)}) copy-start(bf16[512,128]{1,0:T(8,128)(2,1)} %param.11) | copy-start | bytes 393220
  274.7 24.2 %copy-start.1 = (f32[1,512]{1,0:T(1,128)}, f32[1,512]{1,0:T(1,128)S(1)}, u32[]{:S(2)}) copy-start(f32[1,512]{1,0:T(1,128)S(1)} %constant_dynamic-slice_fusion.2) | copy-start | bytes 6148
  278.9 12.1 %all-to-all-start.4 = ((f32[8,1,64]{2,1,0:T(1,128)}), f32[8,1,64]{2,1,0:T(1,128)S(1)}, u32[]{:S(2)}, u32[]{:S(2)}) async-start(f32[8,1,64]{2,1,0:T(1,128)} %all_to_all.33), calls=%async_computation.5 | async-start | bytes 8192 | tf_op jit(solution)/shard_map/all_to_all | solution.py:135
  291.6 9.7 %all-to-all-start.5 = ((bf16[32,2,128]{2,1,0:T(2,128)(2,1)}), bf16[32,2,128]{2,1,0:T(2,128)(2,1)S(1)}, u32[]{:S(2)}, u32[]{:S(2)}) async-start(bf16[32,2,128]{2,1,0:T(2,128)(2,1)} %stack.2), calls=%async_computation.6 | async-start | bytes 32768 | tf_op jit(solution)/shard_map/all_to_all | solution.py:152
  303.9 45.5 %all-to-all-start.2 = ((f32[8,64,128]{2,1,0:T(8,128)}), f32[8,64,128]{2,1,0:T(8,128)S(1)}, u32[]{:S(2)}, u32[]{:S(2)}) async-start(f32[8,64,128]{2,1,0:T(8,128)} %bitcast.22), calls=%async_computation.3 | async-start | bytes 524288 | tf_op jit(solution)/shard_map/all_to_all | solution.py:126
Sparse Core Ops, SparseCore 0:
  265.6 25.9 reduce-scatter.1
